TPU v7x, 32 devices: a whole 2x2x4 slice. The times are simulated.
32 devices in a mesh: row: 4 (over z), col: 8 (over y, x, core).
Axes of the slice: x: 2, y: 2, z: 4, core: 2. Of those that a mesh axis runs over, the one named last changes fastest.
Arguments:
- ainv_anc: bfloat16 [12288, 12288], P('row', 'col'), may hold values from -6 to 6
- l_panel: bfloat16 [1536, 12288], P('col', 'row'), may hold values from -0.109375 to 0.109375
- diag_inv: float32 [1536, 768], P('col', 'row'), may hold values from -6 to 6
- struct_mask: int32 [2, 96], replicated, may hold values 0 or 1
- pieces: float32 [1536, 32, 128], P(('row', 'col')), may hold values from -6 to 6
- tile_owner: int32 [1536, 1], P(('row', 'col')), may hold values from 0 to 31; in each aligned block of 48 rows (0 to 47, 48 to 95, ...) at most 3 rows name the same one
Outputs:
- ainv_upper: bfloat16 [1536, 12288], P('col', 'row')
- ainv_diag: float32 [1536, 768], P('col', 'row')
- moved: float32 [3072, 32, 128], P(('row', 'col'))
Inputs may be any that keep to these rules, and one draw needn't show every extreme that they name: `tile_owner`: among the 48 pieces of one device no owner is named more than 3 times, a bound that some block reaches.
All inputs are finite; a program needn't handle non-finite values.
Results may differ from a plain program's by a relative error of at most 0.015.
Values may be sent and summed in bfloat16 or wider, within the bound.
A program may use at most 128 MiB of HBM per device.

v0:
```python
import jax
import jax.numpy as jnp
from jax import lax
from jax.sharding import PartitionSpec as P

W = 768
AB = 128
SLOT = 3


def broadcast(value, axis, root):
    mine = lax.axis_index(axis) == root
    return lax.psum(jnp.where(mine, value, jnp.zeros_like(value)), axis)


def local(ainv_anc, l_panel, diag_inv, struct_mask, pieces, tile_owner):
    row_devices = lax.axis_size("row")
    col_devices = lax.axis_size("col")
    row_index = lax.axis_index("row")
    col_index = lax.axis_index("col")
    slab_rows = l_panel.shape[0]
    local_rows = l_panel.shape[1]
    cross_width = ainv_anc.shape[1]
    group_ratio = col_devices // row_devices
    supernode = col_index * slab_rows // W
    block_count = local_rows // AB
    keep_blocks = lax.dynamic_slice(
        struct_mask, (supernode, row_index * block_count), (1, block_count)
    )
    keep_rows = (
        jnp.broadcast_to(keep_blocks[:, :, None], (1, block_count, AB)).reshape(1, local_rows) > 0
    )
    masked = jnp.where(keep_rows, l_panel, jnp.zeros_like(l_panel))
    gathered = lax.all_gather(masked, "col", axis=0, tiled=True)
    offset = col_index % group_ratio * cross_width
    own_cross = lax.dynamic_slice_in_dim(gathered, offset, cross_width, 1)
    cross_rows = broadcast(own_cross, "row", col_index // group_ratio)
    product = lax.psum_scatter(
        lax.dot_general(
            cross_rows, ainv_anc, (((1,), (1,)), ((), ())), preferred_element_type=jnp.float32
        ).astype(jnp.bfloat16),
        "col",
        scatter_dimension=0,
        tiled=True,
    ).astype(jnp.float32)
    upper_rows = jnp.where(keep_rows, -product, jnp.zeros_like(product)).astype(jnp.bfloat16)
    own_block = lax.dynamic_slice_in_dim(gathered, supernode * W, W, 0)
    diag_part = lax.dot_general(
        upper_rows, own_block, (((1,), (1,)), ((), ())), preferred_element_type=jnp.float32
    )
    summed = lax.psum_scatter(
        diag_part.astype(jnp.bfloat16), "row", scatter_dimension=1, tiled=True
    ).astype(jnp.float32)
    ainv_diag = diag_inv - summed
    devices_all = row_devices * col_devices
    owners = tile_owner[:, 0]
    onehot = (owners[:, None] == jnp.arange(devices_all, dtype=jnp.int32)[None, :]).astype(
        jnp.int32
    )
    earlier = jnp.cumsum(onehot, axis=0) - onehot
    rank_in_dest = jnp.sum(earlier * onehot, axis=1)
    slot_index = owners * SLOT + rank_in_dest
    piece_rows = pieces.shape[1]
    piece_cols = pieces.shape[2]
    buffer = (
        jnp.zeros((devices_all * SLOT, piece_rows, piece_cols), jnp.float32)
        .at[slot_index]
        .set(pieces)
    )
    shaped = buffer.reshape(devices_all, SLOT, piece_rows, piece_cols)
    arrived = lax.all_to_all(
        shaped.astype(jnp.bfloat16), ("row", "col"), split_axis=0, concat_axis=0, tiled=True
    ).astype(shaped.dtype)
    moved_pieces = arrived.reshape(devices_all * SLOT, piece_rows, piece_cols)
    return (upper_rows, ainv_diag, moved_pieces)


def solution(mesh):
    in_specs = (
        P("row", "col"),
        P("col", "row"),
        P("col", "row"),
        P(),
        P(("row", "col"), None, None),
        P(("row", "col"), None),
    )
    out_specs = (P("col", "row"), P("col", "row"), P(("row", "col"), None, None))
    return jax.shard_map(local, mesh=mesh, in_specs=in_specs, out_specs=out_specs, check_vma=False)
```

profile of v0, /device:TPU:0, one launch (start us, length us, event | category | flops | bytes accessed | tf_op | source)
XLA Modules:
  0.0 382.2 jit_solution(5946898883278234848)
XLA Ops:
  7.2 0.0 all-gather.2.cloned.1.call-start
  7.2 0.8 compare_bitcast_fusion
  8.0 0.1 broadcast_bitcast_fusion
  8.1 2.4 broadcast_select_fusion
  10.5 0.0 all-gather.2.cloned.1.call-update
  10.5 0.0 all-reduce.2.cloned.1.call-start
  10.6 61.5 %all-gather.2.cloned.1.call-done = bf16[1536,3072]{1,0:T(8,128)(2,1)} async-done(((bf16[192,3072]{1,0:T(8,128)(2,1)}), bf16[1536,3072]{1,0:T(8,128)(2,1)}) %all-gather.2.cloned.1.call-update) | async-done | bytes 9437200 | tf_op jit(solution)/shard_map/all_gather | solution.py:34
  72.1 5.4 %dynamic-slice_select_fusion = bf16[1536,1536]{1,0:T(8,128)(2,1)} fusion(bf16[1536,3072]{1,0:T(8,128)(2,1)} %all-gather.2.cloned.1.call-done, s32[]{:T(128)S(6)} %select_n.53, pred[]{:T(512)S(6)} %eq.20), kind=kLoop, calls=%fused_computation.4 | loop fusion | flops 2359296 | bytes 9437189 | tf_op jit(solution)/shard_map/jit(_where)/select_n | solution.py:13
  77.4 0.0 all-reduce.2.cloned.1.call-update
  77.5 0.0 reduce-scatter.5.cloned.1.call-start
  77.5 172.1 %all-reduce.2.cloned.1.call-done = bf16[1536,1536]{1,0:T(8,128)(2,1)} async-done(((bf16[1536,1536]{1,0:T(8,128)(2,1)}), bf16[1536,1536]{1,0:T(8,128)(2,1)}) %all-reduce.2.cloned.1.call-update) | async-done | bytes 4718608 | tf_op jit(solution)/shard_map/psum | solution.py:13
  249.6 20.5 %convolution_convert_fusion = bf16[1536,3072]{1,0:T(8,128)(2,1)} fusion(bf16[1536,1536]{1,0:T(8,128)(2,1)} %all-reduce.2.cloned.1.call-done, bf16[3072,1536]{1,0:T(8,128)(2,1)} %param.6), kind=kOutput, calls=%fused_computation.1 | convolution fusion | flops 14500233216 | bytes 23592960 | tf_op jit(solution)/shard_map/dot_general | solution.py:39
  270.1 0.0 copy-start.3
  270.1 0.0 copy-start.1
  270.1 0.0 reduce-scatter.5.cloned.1.call-update
  270.1 0.6 copy-done.3
  270.7 0.1 fusion.5
  270.8 0.1 reduce_window_sum.11
  270.9 0.2 select_reduce_fusion
  271.1 0.2 broadcast_in_dim.39
  271.2 0.0 copy-done.1
  271.3 2.0 scatter_fusion
  273.3 1.0 convert_element_type.31
  274.3 3.6 all-to-all-start
  277.9 0.0 reduce-scatter.7.cloned.1.call-start
  277.9 68.1 %reduce-scatter.5.cloned.1.call-done = bf16[192,3072]{1,0:T(8,128)(2,1)} async-done(((bf16[1536,3072]{1,0:T(8,128)(2,1)}), bf16[192,3072]{1,0:T(8,128)(2,1)}) %reduce-scatter.5.cloned.1.call-update) | async-done | bytes 1179664 | tf_op jit(solution)/shard_map/reduce_scatter | solution.py:38
  346.0 1.6 select_convert_fusion
  347.6 0.0 copy-start
  347.6 4.5 %fusion.2 = bf16[192,768]{1,0:T(8,128)(2,1)S(1)} fusion(bf16[192,3072]{1,0:T(8,128)(2,1)S(1)} %select_convert_fusion, bf16[1536,3072]{1,0:T(8,128)(2,1)} %all-gather.2.cloned.1.call-done, s32[]{:T(128)S(6)} %select_n.56), kind=kOutput, calls=%fused_computation.6 | convolution fusion | flops 906117120 | bytes 6193156 | tf_op jit(solution)/shard_map/dot_general | solution.py:48
  352.1 0.0 copy-done
  352.1 0.0 copy-start.2
  352.1 0.9 copy.9
  353.0 0.0 reduce-scatter.7.cloned.1.call-update
  353.0 0.0 all-to-all-done
  353.1 1.4 bitcast_convert_fusion
  354.5 19.5 %reduce-scatter.7.cloned.1.call-done = bf16[192,192]{1,0:T(8,128)(2,1)} async-done(((bf16[768,192]{1,0:T(8,128)(2,1)}), bf16[192,192]{1,0:T(8,128)(2,1)}) %reduce-scatter.7.cloned.1.call-update) | async-done | bytes 73744
  374.0 1.0 copy.10
  375.0 0.0 copy-done.2
  375.0 0.7 convert_subtract_fusion
  (1 shorter events, 0.0 us)
Async XLA Ops:
  7.2 64.9 %all-gather.2.cloned.1.call-start = ((), (), s32[]{:S(2)}) async-start(), calls=%async_computation.3 | async-start | bytes 10616832 | tf_op jit(solution)/shard_map/all_gather | solution.py:34
  10.5 239.1 %all-reduce.2.cloned.1.call-start = ((), (), s32[]{:S(2)}) async-start(), calls=%async_computation.4 | async-start | bytes 9437184 | tf_op jit(solution)/shard_map/psum | solution.py:13
  77.5 268.6 %reduce-scatter.5.cloned.1.call-start = ((), (), s32[]{:S(2)}) async-start(), calls=%async_computation.5 | async-start | bytes 10616832 | tf_op jit(solution)/shard_map/reduce_scatter | solution.py:38
  270.1 0.7 copy-start.3
  270.1 1.2 copy-start.1
  274.3 78.7 %all-to-all-start = ((bf16[32,3,32,128]{3,2,1,0:T(8,128)(2,1)}), bf16[32,3,32,128]{3,2,1,0:T(8,128)(2,1)S(1)}, u32[]{:S(2)}, u32[]{:S(2)}) async-start(bf16[32,3,32,128]{3,2,1,0:T(8,128)(2,1)} %bitcast.5), calls=%async_computation.1 | async-start | bytes 1572864 | tf_op jit(solution)/shard_map/all_to_all | solution.py:71
  277.9 96.1 %reduce-scatter.7.cloned.1.call-start = ((), (), s32[]{:S(2)}) async-start(), calls=%async_computation.6 | async-start | bytes 491520
  347.6 4.5 %copy-start = (bf16[192,3072]{1,0:T(8,128)(2,1)}, bf16[192,3072]{1,0:T(8,128)(2,1)S(1)}, u32[]{:S(2)}) copy-start(bf16[192,3072]{1,0:T(8,128)(2,1)S(1)} %select_convert_fusion) | copy-start | bytes 3538948
  352.1 22.9 %copy-start.2 = (f32[192,192]{1,0:T(8,128)S(1)}, f32[192,192]{1,0:T(8,128)}, u32[]{:S(2)}) copy-start(f32[192,192]{1,0:T(8,128)} %param.8) | copy-start | bytes 442372
Sparse Core Ops, SparseCore 0:
  10.6 61.4 all-gather.1
  77.6 171.9 all-reduce.1
  270.2 75.7 reduce-scatter.4
  353.2 20.7 reduce-scatter.6
where the time goes:
time: 383 us; the launch traced here: 382 us
  waiting for transfers between devices  321 us (84%)
  matrix products  25 us (7%)
  between operations  13.9 us (4%)
  other arithmetic  13.6 us (4%)
  local copies, waits for them, and re-layouts  4.82 us (1%)
    psum x1, waiting for transfers between devices, broadcast(): return lax.psum(jnp.where(mine, value, jnp.zeros_like(value)), axis)  172 us
    reduce_scatter x1, waiting for transfers between devices, local(): lax.psum_scatter(lax.dot_general(cross_rows, ainv_anc, (((1,), (1,)), (()...  68.1 us
    all_gather x1, waiting for transfers between devices, local(): gathered = lax.all_gather(masked, 'col', axis=0, tiled=True)  61.5 us
    dot_general x1, matrix products, local(): lax.dot_general(cross_rows, ainv_anc, (((1,), (1,)), ((), ())), preferred...  20.5 us
    unnamed x5, waiting for transfers between devices  19.6 us
  transfers between devices with their start and end apart: 5, of which 4 were waited for; matrix products, arithmetic and copies ran while one was open for 3% of the time, Pallas kernels for 0%

commit v1 on v0

--- a/solution.py
+++ b/solution.py
@@ -31,7 +31,12 @@
         jnp.broadcast_to(keep_blocks[:, :, None], (1, block_count, AB)).reshape(1, local_rows) > 0
     )
     masked = jnp.where(keep_rows, l_panel, jnp.zeros_like(l_panel))
-    gathered = lax.all_gather(masked, "col", axis=0, tiled=True)
+    ring = [masked]
+    for hop in range(7):
+        ring.append(lax.ppermute(ring[-1], "col", [(dev, (dev + 1) % 8) for dev in range(8)]))
+    gathered = jnp.roll(
+        jnp.concatenate(ring[::-1], axis=0), (lax.axis_index("col") + 1) * ring[0].shape[0], axis=0
+    )
     offset = col_index % group_ratio * cross_width
     own_cross = lax.dynamic_slice_in_dim(gathered, offset, cross_width, 1)
     cross_rows = broadcast(own_cross, "row", col_index // group_ratio)

time: 383 us -> 454 us (1.19)
  waiting for transfers between devices: 321 us -> 377 us
  local copies, waits for them, and re-layouts: 4.82 us -> 20.4 us
    ppermute x0 -> x7, waiting for transfers between devices: none -> 116 us  [local(): lax.ppermute(ring[-1], 'col', [(dev, (dev + 1) % 8) for dev in range(8)])]
    all_gather x1 -> x0, waiting for transfers between devices: 61.5 us -> none  [local(): gathered = lax.all_gather(masked, 'col', axis=0, tiled=True)]
    unnamed x10 -> x36, local copies, waits for them, and re-layouts: 2.55 us -> 18.1 us
    unnamed x5 -> x4, waiting for transfers between devices: 19.6 us -> 19.6 us
  transfers between devices with their start and end apart: 5 -> 11, of which waited for: 4 -> 10; matrix products, arithmetic and copies ran while one was open for 3% -> 3% of each run, Pallas kernels for 0% -> 0%
where the time goes in v1:
time: 454 us
  waiting for transfers between devices  377 us (83%)
  matrix products  25.1 us (6%)
  local copies, waits for them, and re-layouts  20.4 us (4%)
  between operations  14 us (3%)
  other arithmetic  12.8 us (3%)
    psum x1, waiting for transfers between devices, broadcast(): return lax.psum(jnp.where(mine, value, jnp.zeros_like(value)), axis)  173 us
    ppermute x7, waiting for transfers between devices, local(): lax.ppermute(ring[-1], 'col', [(dev, (dev + 1) % 8) for dev in range(8)])  116 us
    reduce_scatter x1, waiting for transfers between devices, local(): lax.psum_scatter(lax.dot_general(cross_rows, ainv_anc, (((1,), (1,)), (()...  68.1 us
    dot_general x1, matrix products, local(): lax.dot_general(cross_rows, ainv_anc, (((1,), (1,)), ((), ())), preferred...  20.5 us
    unnamed x4, waiting for transfers between devices  19.6 us
    unnamed x36, local copies, waits for them, and re-layouts  18.1 us
  transfers between devices with their start and end apart: 11, of which 10 were waited for; matrix products, arithmetic and copies ran while one was open for 3% of the time, Pallas kernels for 0%

profile of v1, /device:TPU:0, one launch (start us, length us, event | category | flops | bytes accessed | tf_op | source)
XLA Modules:
  0.0 453.7 jit_solution(5319764674192437781)
XLA Ops:
  7.2 0.8 compare_bitcast_fusion
  8.0 0.1 broadcast_bitcast_fusion
  8.1 1.4 broadcast_select_fusion
  9.4 0.5 collective-permute-start
  10.0 16.8 %collective-permute-done = bf16[192,3072]{1,0:T(8,128)(2,1)S(1)} collective-permute-done((bf16[192,3072]{1,0:T(8,128)(2,1)S(1)}, bf16[192,3072]{1,0:T(8,128)(2,1)S(1)}, u32[]{:S(2)}, u32[]{:S(2)}) %collective-permute-start) | collective-permute-done | bytes 1179680 | tf_op jit(solution)/shard_map/ppermute | solution.py:36
  26.7 16.5 %collective-permute-done.1 = bf16[192,3072]{1,0:T(8,128)(2,1)S(1)} collective-permute-done((bf16[192,3072]{1,0:T(8,128)(2,1)S(1)}, bf16[192,3072]{1,0:T(8,128)(2,1)S(1)}, u32[]{:S(2)}, u32[]{:S(2)}) %collective-permute-start.1) | collective-permute-done | bytes 1179680 | tf_op jit(solution)/shard_map/ppermute | solution.py:36
  43.3 16.5 %collective-permute-done.2 = bf16[192,3072]{1,0:T(8,128)(2,1)S(1)} collective-permute-done((bf16[192,3072]{1,0:T(8,128)(2,1)S(1)}, bf16[192,3072]{1,0:T(8,128)(2,1)S(1)}, u32[]{:S(2)}, u32[]{:S(2)}) %collective-permute-start.2) | collective-permute-done | bytes 1179680 | tf_op jit(solution)/shard_map/ppermute | solution.py:36
  59.8 16.5 %collective-permute-done.3 = bf16[192,3072]{1,0:T(8,128)(2,1)S(1)} collective-permute-done((bf16[192,3072]{1,0:T(8,128)(2,1)S(1)}, bf16[192,3072]{1,0:T(8,128)(2,1)S(1)}, u32[]{:S(2)}, u32[]{:S(2)}) %collective-permute-start.3) | collective-permute-done | bytes 1179680 | tf_op jit(solution)/shard_map/ppermute | solution.py:36
  76.3 1.0 copy-done.1
  77.3 16.5 %collective-permute-done.4 = bf16[192,3072]{1,0:T(8,128)(2,1)S(1)} collective-permute-done((bf16[192,3072]{1,0:T(8,128)(2,1)S(1)}, bf16[192,3072]{1,0:T(8,128)(2,1)S(1)}, u32[]{:S(2)}, u32[]{:S(2)}) %collective-permute-start.4) | collective-permute-done | bytes 1179680 | tf_op jit(solution)/shard_map/ppermute | solution.py:36
  93.9 1.0 copy-done.3
  94.9 16.6 %collective-permute-done.5 = bf16[192,3072]{1,0:T(8,128)(2,1)} collective-permute-done((bf16[192,3072]{1,0:T(8,128)(2,1)S(1)}, bf16[192,3072]{1,0:T(8,128)(2,1)}, u32[]{:S(2)}, u32[]{:S(2)}) %collective-permute-start.5) | collective-permute-done | bytes 1179680 | tf_op jit(solution)/shard_map/ppermute | solution.py:36
  111.5 16.8 %collective-permute-done.6 = bf16[192,3072]{1,0:T(8,128)(2,1)} collective-permute-done((bf16[192,3072]{1,0:T(8,128)(2,1)}, bf16[192,3072]{1,0:T(8,128)(2,1)}, u32[]{:S(2)}, u32[]{:S(2)}) %collective-permute-start.6) | collective-permute-done | bytes 1179680 | tf_op jit(solution)/shard_map/ppermute | solution.py:36
  128.4 1.3 constant_dynamic-update-slice_fusion.15
  129.7 1.3 constant_dynamic-update-slice_fusion.14
  131.1 0.1 constant_dynamic-update-slice_fusion.13
  131.2 0.1 constant_dynamic-update-slice_fusion.12
  131.3 0.1 constant_dynamic-update-slice_fusion.11
  131.4 0.1 constant_dynamic-update-slice_fusion.10
  131.4 0.1 constant_dynamic-update-slice_fusion.9
  131.5 0.9 copy-done
  132.4 0.2 constant_dynamic-update-slice_fusion.8
  132.7 1.3 constant_dynamic-update-slice_fusion.7
  134.0 1.3 constant_dynamic-update-slice_fusion.6
  135.4 0.1 constant_dynamic-update-slice_fusion.5
  135.5 0.1 constant_dynamic-update-slice_fusion.4
  135.6 0.1 constant_dynamic-update-slice_fusion.3
  135.6 0.1 constant_dynamic-update-slice_fusion.2
  135.7 0.1 constant_dynamic-update-slice_fusion.1
  135.8 0.2 constant_dynamic-update-slice_fusion
  136.1 6.5 %copy-done.5 = bf16[3072,3072]{1,0:T(8,128)(2,1)} copy-done((bf16[3072,3072]{1,0:T(8,128)(2,1)}, bf16[3072,3072]{1,0:T(8,128)(2,1)S(1)}, u32[]{:S(2)}) %copy-start.5) | copy-done | bytes 18874392
  142.5 5.2 %dynamic-slice_select_fusion = bf16[1536,1536]{1,0:T(8,128)(2,1)} fusion(bf16[3072,3072]{1,0:T(8,128)(2,1)S(1)} %constant_dynamic-update-slice_fusion, s32[]{:T(128)S(6)} %select_n.72, s32[]{:T(128)S(6)} %select_n.75, pred[]{:T(512)S(6)} %eq.23), kind=kLoop, calls=%fused_computation.4 | loop fusion | flops 2359296 | bytes 9437193 | tf_op jit(solution)/shard_map/jit(_where)/select_n | solution.py:13
  147.8 173.1 %all-reduce.2.cloned.1.call-done = bf16[1536,1536]{1,0:T(8,128)(2,1)} async-done(((bf16[1536,1536]{1,0:T(8,128)(2,1)}), bf16[1536,1536]{1,0:T(8,128)(2,1)}) %all-reduce.2.cloned.1.call-update) | async-done | bytes 4718608 | tf_op jit(solution)/shard_map/psum | solution.py:13
  320.9 20.5 %convolution_convert_fusion = bf16[1536,3072]{1,0:T(8,128)(2,1)} fusion(bf16[1536,1536]{1,0:T(8,128)(2,1)} %all-reduce.2.cloned.1.call-done, bf16[3072,1536]{1,0:T(8,128)(2,1)} %param.6), kind=kOutput, calls=%fused_computation.1 | convolution fusion | flops 14500233216 | bytes 23592960 | tf_op jit(solution)/shard_map/dot_general | solution.py:44
  341.5 0.6 copy-done.9
  342.3 0.2 select_reduce_fusion
  342.5 0.2 broadcast_in_dim.39
  342.7 2.0 scatter_fusion
  344.7 1.0 convert_element_type.31
  345.7 3.6 all-to-all-start
  349.4 68.1 %reduce-scatter.5.cloned.1.call-done = bf16[192,3072]{1,0:T(8,128)(2,1)} async-done(((bf16[1536,3072]{1,0:T(8,128)(2,1)}), bf16[192,3072]{1,0:T(8,128)(2,1)}) %reduce-scatter.5.cloned.1.call-update) | async-done | bytes 1179664 | tf_op jit(solution)/shard_map/reduce_scatter | solution.py:43
  417.4 1.6 select_convert_fusion
  419.0 4.5 fusion.2
  423.5 0.9 copy.9
  424.5 1.4 bitcast_convert_fusion
  425.9 19.5 %reduce-scatter.7.cloned.1.call-done = bf16[192,192]{1,0:T(8,128)(2,1)} async-done(((bf16[768,192]{1,0:T(8,128)(2,1)}), bf16[192,192]{1,0:T(8,128)(2,1)}) %reduce-scatter.7.cloned.1.call-update) | async-done | bytes 73744
  445.4 1.0 copy.10
  446.5 0.7 convert_subtract_fusion
  (31 shorter events, 0.4 us)
Async XLA Ops:
  7.2 313.8 %all-reduce.2.cloned.1.call-start = ((), (), s32[]{:S(2)}) async-start(), calls=%async_computation.3 | async-start | bytes 9437184 | tf_op jit(solution)/shard_map/psum | solution.py:13
  9.4 17.3 %collective-permute-start = (bf16[192,3072]{1,0:T(8,128)(2,1)S(1)}, bf16[192,3072]{1,0:T(8,128)(2,1)S(1)}, u32[]{:S(2)}, u32[]{:S(2)}) collective-permute-start(bf16[192,3072]{1,0:T(8,128)(2,1)S(1)} %broadcast_select_fusion), channel_id=1, source_target_pairs={{0,1},{1,2},{2,3},{3,4},{4,5},{5,6},{6,7},{7,0},{8,9},{9,10},{10,1... | collective-permute-start | bytes 3538952 | tf_op jit(solution)/shard_map/ppermute | solution.py:36
  26.7 16.5 %collective-permute-start.1 = (bf16[192,3072]{1,0:T(8,128)(2,1)S(1)}, bf16[192,3072]{1,0:T(8,128)(2,1)S(1)}, u32[]{:S(2)}, u32[]{:S(2)}) collective-permute-start(bf16[192,3072]{1,0:T(8,128)(2,1)S(1)} %collective-permute-done), channel_id=1, source_target_pairs={{0,1},{1,2},{2,3},{3,4},{4,5},{5,6},{6,7},{7,0},{8,9},{9,10},{10,1... | collective-permute-start | bytes 3538952 | tf_op jit(solution)/shard_map/ppermute | solution.py:36
  43.3 16.5 %collective-permute-start.2 = (bf16[192,3072]{1,0:T(8,128)(2,1)S(1)}, bf16[192,3072]{1,0:T(8,128)(2,1)S(1)}, u32[]{:S(2)}, u32[]{:S(2)}) collective-permute-start(bf16[192,3072]{1,0:T(8,128)(2,1)S(1)} %collective-permute-done.1), channel_id=1, source_target_pairs={{0,1},{1,2},{2,3},{3,4},{4,5},{5,6},{6,7},{7,0},{8,9},{9,10},{10,1... | collective-permute-start | bytes 3538952 | tf_op jit(solution)/shard_map/ppermute | solution.py:36
  59.8 16.5 %collective-permute-start.3 = (bf16[192,3072]{1,0:T(8,128)(2,1)S(1)}, bf16[192,3072]{1,0:T(8,128)(2,1)S(1)}, u32[]{:S(2)}, u32[]{:S(2)}) collective-permute-start(bf16[192,3072]{1,0:T(8,128)(2,1)S(1)} %collective-permute-done.2), channel_id=1, source_target_pairs={{0,1},{1,2},{2,3},{3,4},{4,5},{5,6},{6,7},{7,0},{8,9},{9,10},{10,1... | collective-permute-start | bytes 3538952 | tf_op jit(solution)/shard_map/ppermute | solution.py:36
  76.3 1.0 copy-start.1
  77.3 16.5 %collective-permute-start.4 = (bf16[192,3072]{1,0:T(8,128)(2,1)S(1)}, bf16[192,3072]{1,0:T(8,128)(2,1)S(1)}, u32[]{:S(2)}, u32[]{:S(2)}) collective-permute-start(bf16[192,3072]{1,0:T(8,128)(2,1)S(1)} %collective-permute-done.3), channel_id=1, source_target_pairs={{0,1},{1,2},{2,3},{3,4},{4,5},{5,6},{6,7},{7,0},{8,9},{9,10},{10,1... | collective-permute-start | bytes 3538952 | tf_op jit(solution)/shard_map/ppermute | solution.py:36
  93.9 1.0 copy-start.3
  94.9 16.6 %collective-permute-start.5 = (bf16[192,3072]{1,0:T(8,128)(2,1)S(1)}, bf16[192,3072]{1,0:T(8,128)(2,1)}, u32[]{:S(2)}, u32[]{:S(2)}) collective-permute-start(bf16[192,3072]{1,0:T(8,128)(2,1)S(1)} %collective-permute-done.4), channel_id=1, source_target_pairs={{0,1},{1,2},{2,3},{3,4},{4,5},{5,6},{6,7},{7,0},{8,9},{9,10},{10,1... | collective-permute-start | bytes 3538952 | tf_op jit(solution)/shard_map/ppermute | solution.py:36
  111.5 16.8 %collective-permute-start.6 = (bf16[192,3072]{1,0:T(8,128)(2,1)}, bf16[192,3072]{1,0:T(8,128)(2,1)}, u32[]{:S(2)}, u32[]{:S(2)}) collective-permute-start(bf16[192,3072]{1,0:T(8,128)(2,1)} %collective-permute-done.5), channel_id=1, source_target_pairs={{0,1},{1,2},{2,3},{3,4},{4,5},{5,6},{6,7},{7,0},{8,9},{9,10},{10,1... | collective-permute-start | bytes 3538952 | tf_op jit(solution)/shard_map/ppermute | solution.py:36
  111.5 19.5 %copy-start.4 = (bf16[192,3072]{1,0:T(8,128)(2,1)S(1)}, bf16[192,3072]{1,0:T(8,128)(2,1)}, u32[]{:S(2)}) copy-start(bf16[192,3072]{1,0:T(8,128)(2,1)} %copy-done.3) | copy-start | bytes 3538948
  111.5 19.6 %copy-start.2 = (bf16[192,3072]{1,0:T(8,128)(2,1)S(1)}, bf16[192,3072]{1,0:T(8,128)(2,1)}, u32[]{:S(2)}) copy-start(bf16[192,3072]{1,0:T(8,128)(2,1)} %copy-done.1) | copy-start | bytes 3538948
  131.2 1.3 copy-start
  136.1 6.5 %copy-start.5 = (bf16[3072,3072]{1,0:T(8,128)(2,1)}, bf16[3072,3072]{1,0:T(8,128)(2,1)S(1)}, u32[]{:S(2)}) copy-start(bf16[3072,3072]{1,0:T(8,128)(2,1)S(1)} %constant_dynamic-update-slice_fusion) | copy-start | bytes 56623108
  147.8 269.7 %reduce-scatter.5.cloned.1.call-start = ((), (), s32[]{:S(2)}) async-start(), calls=%async_computation.4 | async-start | bytes 10616832 | tf_op jit(solution)/shard_map/reduce_scatter | solution.py:43
  341.5 0.7 copy-start.9
  341.5 1.2 copy-start.7
  345.7 78.7 %all-to-all-start = ((bf16[32,3,32,128]{3,2,1,0:T(8,128)(2,1)}), bf16[32,3,32,128]{3,2,1,0:T(8,128)(2,1)S(1)}, u32[]{:S(2)}, u32[]{:S(2)}) async-start(bf16[32,3,32,128]{3,2,1,0:T(8,128)(2,1)} %bitcast.5), calls=%async_computation.1 | async-start | bytes 1572864 | tf_op jit(solution)/shard_map/all_to_all | solution.py:76
  349.3 96.2 %reduce-scatter.7.cloned.1.call-start = ((), (), s32[]{:S(2)}) async-start(), calls=%async_computation.5 | async-start | bytes 491520
  419.0 6.9 %copy-start.6 = (bf16[192,3072]{1,0:T(8,128)(2,1)}, bf16[192,3072]{1,0:T(8,128)(2,1)S(1)}, u32[]{:S(2)}) copy-start(bf16[192,3072]{1,0:T(8,128)(2,1)S(1)} %select_convert_fusion) | copy-start | bytes 3538948
  419.0 27.4 %copy-start.8 = (f32[192,192]{1,0:T(8,128)S(1)}, f32[192,192]{1,0:T(8,128)}, u32[]{:S(2)}) copy-start(f32[192,192]{1,0:T(8,128)} %param.8) | copy-start | bytes 442372
Sparse Core Ops, SparseCore 0:
  147.9 173.0 all-reduce.1
  341.6 75.7 reduce-scatter.4
  424.6 20.8 reduce-scatter.6
